TPU v7x, 32 devices: a whole 2x2x4 slice. The times are simulated.
32 devices in a mesh: row: 4 (over y, x), col: 8 (over z, core).
Axes of the slice: x: 2, y: 2, z: 4, core: 2. Of those that a mesh axis runs over, the one named last changes fastest.
Arguments:
- activations: bfloat16 [1024, 9216], P('col', 'row'), may hold values from -64 to 64
- output_grads: bfloat16 [1024, 73728], P('row', 'col'), may hold values from -16 to 16
- weight: bfloat16 [9216, 73728], P('row', 'col'), may hold values from -1 to 1
- row_moment: float32 [9216], P('row'), may hold values from 0.01 to 0.3
- col_moment: float32 [73728], P('col'), may hold values from 0.01 to 0.3
Outputs:
- new_weight: bfloat16 [9216, 73728], P('row', 'col')
- new_row: float32 [9216], P('row')
- new_col: float32 [73728], P('col')
All inputs are finite; a program needn't handle non-finite values.
Results may differ from a plain program's by a relative error of at most 0.0004.
Values may be sent and summed in bfloat16 or wider, within the bound.
No kernel may reach another device: no remote copies, remote signals or barrier semaphores. Data moves between devices by JAX's collectives and lax.ppermute only.
A program may use at most 256 MiB of HBM per device.

v0:
```python
import jax
import jax.numpy as jnp
from jax import lax
from jax.sharding import PartitionSpec as P

ADDED_SQUARE = 1e-30
DECAY_RATE = 0.8
CLIP_LIMIT = 1.0
STEP_SIZE = 0.1
MEAN_OFFSET = 1e-06


def on_device(activations, output_grads, weight, row_moment, col_moment):
    tile_rows, tile_cols = weight.shape
    total_rows = tile_rows * lax.axis_size("row")
    total_cols = tile_cols * lax.axis_size("col")
    entries = float(total_rows * total_cols)
    weight_wide = weight.astype(jnp.float32)
    weight_local = jnp.sum(weight_wide * weight_wide)
    weight_total = lax.psum(weight_local, ("row", "col"))
    contract = (((0,), (0,)), ((), ()))
    acts_all = lax.all_gather(activations, "col", axis=0, tiled=True)
    gradient = lax.dot_general(
        acts_all,
        lax.all_gather(output_grads, "row", axis=0, tiled=True),
        contract,
        preferred_element_type=jnp.float32,
    )
    squared = gradient * gradient
    row_part = jnp.sum(squared + ADDED_SQUARE, axis=1)
    col_part = jnp.sum(squared + ADDED_SQUARE, axis=0)
    row_total = lax.psum(row_part, "col")
    col_total = lax.psum(col_part, "row")
    new_row = DECAY_RATE * row_moment + (1.0 - DECAY_RATE) * row_total / total_cols
    new_col = DECAY_RATE * col_moment + (1.0 - DECAY_RATE) * col_total / total_rows
    inverse = lax.rsqrt(new_row[:, None] * new_col[None, :])
    ratio_local = jnp.sum(squared * inverse * inverse)
    leader = (lax.axis_index("col") == 0).astype(jnp.float32)
    row_local = leader * jnp.sum(new_row)
    row_sum, ratio_sum = lax.psum((row_local, ratio_local), ("row", "col"))
    row_mean = row_sum / total_rows
    rms_update = jnp.sqrt(row_mean * ratio_sum / entries)
    clip_factor = jnp.maximum(1.0, rms_update / CLIP_LIMIT)
    step_scale = STEP_SIZE * jnp.sqrt(weight_total / entries + MEAN_OFFSET)
    update = gradient * inverse * jnp.sqrt(row_mean)
    new_weight = (weight_wide - step_scale / clip_factor * update).astype(jnp.bfloat16)
    return (new_weight, new_row, new_col)


def solution(mesh):
    return jax.shard_map(
        on_device,
        mesh=mesh,
        in_specs=(P("col", "row"), P("row", "col"), P("row", "col"), P("row"), P("col")),
        out_specs=(P("row", "col"), P("row"), P("col")),
        check_vma=False,
    )
```

profile of v0, /device:TPU:12, one launch (start us, length us, event | category | flops | bytes accessed | tf_op | source)
XLA Modules:
  0.0 471.2 jit_solution(5277439258976595096)
XLA Ops:
  7.2 0.0 all-gather.3.cloned.1.call-start
  7.2 0.7 all-gather.3.cloned.1.call-update
  7.9 0.0 all-gather.5.cloned.1.call-start
  7.9 0.7 all-gather.5.cloned.1.call-update
  8.7 24.5 %fusion = f32[]{:T(128)} fusion(bf16[2304,9216]{1,0:T(8,128)(2,1)} %param.7), kind=kLoop, calls=%fused_computation.3 | loop fusion | flops 63700992 | bytes 42467332 | tf_op jit(solution)/shard_map/reduce_sum | solution.py:19
  33.1 0.0 copy-start.2
  33.2 0.0 copy-start.3
  33.2 27.4 %all-gather.3.cloned.1.call-done = bf16[1024,2304]{1,0:T(8,128)(2,1)} async-done(((bf16[128,2304]{1,0:T(8,128)(2,1)}), bf16[1024,2304]{1,0:T(8,128)(2,1)}) %all-gather.3.cloned.1.call-update) | async-done | bytes 4718608 | tf_op jit(solution)/shard_map/all_gather | solution.py:22
  60.5 177.9 %all-gather.5.cloned.1.call-done = bf16[1024,9216]{1,0:T(8,128)(2,1)} async-done(((bf16[256,9216]{1,0:T(8,128)(2,1)}), bf16[1024,9216]{1,0:T(8,128)(2,1)}) %all-gather.5.cloned.1.call-update) | async-done | bytes 18874384 | tf_op jit(solution)/shard_map/all_gather | solution.py:25
  238.4 59.5 %add_reduce_fusion = (f32[9216]{0:T(1024)S(1)}, f32[2304]{0:T(1024)S(1)}, f32[2304,9216]{1,0:T(8,128)}) fusion(bf16[1024,2304]{1,0:T(8,128)(2,1)} %all-gather.3.cloned.1.call-done, bf16[1024,9216]{1,0:T(8,128)(2,1)} %all-gather.5.cloned.1.call-done), kind=kOutput, calls=%fused_computation.7 | convolution fusion | flops 43571466240 | bytes 108573696 | tf_op jit(solution)/shard_map/dot_general | solution.py:23
  297.9 15.7 %psum.38 = f32[9216]{0:T(1024)S(1)} all-reduce(f32[9216]{0:T(1024)S(1)} %get-tuple-element.3), channel_id=1, replica_groups=mesh['row'=4,'col'=8] {'row'}, use_global_device_ids=true, to_apply=%region_7.0 | all-reduce | flops 9216 | bytes 73728 | tf_op jit(solution)/shard_map/psum | solution.py:33
  313.6 22.4 %psum.36 = f32[2304]{0:T(1024)S(1)} all-reduce(f32[2304]{0:T(1024)S(1)} %get-tuple-element.4), channel_id=1, replica_groups=mesh['row'=4,'col'=8] {'col'}, use_global_device_ids=true, to_apply=%region_3.0 | all-reduce | flops 2304 | bytes 18432 | tf_op jit(solution)/shard_map/psum | solution.py:32
  336.0 0.0 copy-done.2
  336.0 0.0 copy-done.3
  336.0 0.0 copy-start
  336.0 0.6 fusion.3
  336.6 0.0 copy-start.1
  336.6 28.1 %fusion.2 = f32[]{:T(128)} fusion(f32[2304,9216]{1,0:T(8,128)} %get-tuple-element.10, f32[9216]{0:T(1024)S(1)} %multiply_add_fusion, f32[2304]{0:T(1024)S(1)} %get-tuple-element.9), kind=kLoop, calls=%fused_computation.5 | loop fusion | flops 106168320 | bytes 84980736 | tf_op jit(solution)/shard_map/reduce_sum | solution.py:37
  365.4 43.2 %all-reduce = (f32[]{:T(128)}, f32[]{:T(128)}, f32[]{:T(128)}) all-reduce(f32[]{:T(128)S(6)} %mul.66, f32[]{:T(128)} %fusion, f32[]{:T(128)} %fusion.2), channel_id=1, replica_groups=mesh['row'=4,'col'=8] {'row','col'}, use_global_device_ids=true, to_apply=%region_5.0 | all-reduce | flops 3 | bytes 24 | tf_op jit(solution)/shard_map/psum | solution.py:40
  410.6 53.7 %fusion.1 = bf16[2304,9216]{1,0:T(8,128)(2,1)} fusion(bf16[2304,9216]{1,0:T(8,128)(2,1)} %param.7, f32[2304,9216]{1,0:T(8,128)} %get-tuple-element.10, f32[]{:T(128)S(6)} %sqrt.11, f32[]{:T(128)S(6)} %div.32, f32[9216]{0:T(1024)S(1)} %multiply_add_fusion, f32[2304]{0:T(1024)S(1)} %get-tuple-element.9), kind=kLoop, calls=%fused_computation.4 | loop fusion | flops 148635648 | bytes 169915392 | tf_op jit(solution)/shard_map/convert_element_type | solution.py:46
  464.3 0.0 copy-done
  464.3 0.0 copy-done.1
  (1 shorter events, 0.0 us)
Async XLA Ops:
  7.2 53.4 %all-gather.3.cloned.1.call-start = ((), (), s32[]{:S(2)}) async-start(), calls=%async_computation | async-start | bytes 5308416 | tf_op jit(solution)/shard_map/all_gather | solution.py:22
  7.9 230.5 %all-gather.5.cloned.1.call-start = ((), (), s32[]{:S(2)}) async-start(), calls=%async_computation.1 | async-start | bytes 23592960 | tf_op jit(solution)/shard_map/all_gather | solution.py:25
  33.1 302.8 %copy-start.2 = (f32[9216]{0:T(1024)S(1)}, f32[9216]{0:T(1024)}, u32[]{:S(2)}) copy-start(f32[9216]{0:T(1024)} %param.9) | copy-start | bytes 110596
  33.2 302.9 %copy-start.3 = (f32[2304]{0:T(1024)S(1)}, f32[2304]{0:T(1024)}, u32[]{:S(2)}) copy-start(f32[2304]{0:T(1024)} %param.8) | copy-start | bytes 27652
  336.0 128.3 %copy-start = (f32[9216]{0:T(1024)}, f32[9216]{0:T(1024)S(1)}, u32[]{:S(2)}) copy-start(f32[9216]{0:T(1024)S(1)} %multiply_add_fusion) | copy-start | bytes 110596
  336.6 127.7 %copy-start.1 = (f32[2304]{0:T(1024)}, f32[2304]{0:T(1024)S(1)}, u32[]{:S(2)}) copy-start(f32[2304]{0:T(1024)S(1)} %get-tuple-element.9) | copy-start | bytes 27652
Sparse Core Ops, SparseCore 0:
  9.6 50.8 all-gather.2
  62.4 175.9 all-gather.4
where the time goes:
time: 472 us; the launch traced here: 471 us
  waiting for transfers between devices  207 us (44%)
  other arithmetic  107 us (23%)
  blocking collectives  81.3 us (17%)
  matrix products  59.5 us (13%)
  between operations  16.8 us (4%)
    all_gather x1, waiting for transfers between devices, on_device(): lax.all_gather(output_grads, 'row', axis=0, tiled=True)  178 us
    dot_general x1, matrix products, on_device(): lax.dot_general(acts_all, lax.all_gather(output_grads, 'row', axis=0, til...  59.5 us
    convert_element_type x1, other arithmetic, on_device(): (weight_wide - step_scale / clip_factor * update).astype(jnp.bfloat16)  53.7 us
    psum x1, blocking collectives, on_device(): row_sum, ratio_sum = lax.psum((row_local, ratio_local), ('row', 'col'))  43.2 us
    reduce_sum x1, other arithmetic, on_device(): ratio_local = jnp.sum(squared * inverse * inverse)  28.1 us
    all_gather x1, waiting for transfers between devices, on_device(): acts_all = lax.all_gather(activations, 'col', axis=0, tiled=True)  27.4 us
    reduce_sum x1, other arithmetic, on_device(): weight_local = jnp.sum(weight_wide * weight_wide)  24.5 us
    psum x1, blocking collectives, on_device(): row_total = lax.psum(row_part, 'col')  22.4 us
  transfers between devices with their start and end apart: 2, of which 2 were waited for; matrix products, arithmetic and copies ran while one was open for 5% of the time, Pallas kernels for 0%

commit v1 on v0

--- a/solution.py
+++ b/solution.py
@@ -19,7 +19,14 @@
     weight_local = jnp.sum(weight_wide * weight_wide)
     weight_total = lax.psum(weight_local, ("row", "col"))
     contract = (((0,), (0,)), ((), ()))
-    acts_all = lax.all_gather(activations, "col", axis=0, tiled=True)
+    size = lax.axis_size("col")
+    hops = [(i, (i + 1) % size) for i in range(size)]
+    pieces = [activations]
+    for reach in range(1, size):
+        pieces = [lax.ppermute(pieces[0], "col", hops), *pieces]
+    full = jnp.concatenate(pieces, axis=0)
+    shift = (lax.axis_index("col") + 1) * pieces[-1].shape[0]
+    acts_all = jnp.roll(full, shift, axis=0)
     gradient = lax.dot_general(
         acts_all,
         lax.all_gather(output_grads, "row", axis=0, tiled=True),

time: 472 us -> 420 us (0.89)
  waiting for transfers between devices: 207 us -> 137 us
  local copies, waits for them, and re-layouts: 0.02 us -> 18.1 us
    all_gather x1, waiting for transfers between devices: 178 us -> 80 us  [on_device(): lax.all_gather(output_grads, 'row', axis=0, tiled=True)]
    ppermute x0 -> x7, waiting for transfers between devices: none -> 56.1 us  [on_device(): pieces = [lax.ppermute(pieces[0], 'col', hops), *pieces]]
    all_gather x1 -> x0, waiting for transfers between devices: 27.4 us -> none  [on_device(): acts_all = lax.all_gather(activations, 'col', axis=0, tiled=True)]
    unnamed x8 -> x25, local copies, waits for them, and re-layouts: 0.02 us -> 17.2 us
  transfers between devices with their start and end apart: 2 -> 8, of which waited for: 2 -> 7; matrix products, arithmetic and copies ran while one was open for 5% -> 10% of each run, Pallas kernels for 0% -> 0%
where the time goes in v1:
time: 420 us
  waiting for transfers between devices  137 us (33%)
  other arithmetic  107 us (25%)
  blocking collectives  81.5 us (19%)
  matrix products  59.5 us (14%)
  local copies, waits for them, and re-layouts  18.1 us (4%)
  between operations  16.8 us (4%)
    all_gather x1, waiting for transfers between devices, on_device(): lax.all_gather(output_grads, 'row', axis=0, tiled=True)  80 us
    dot_general x1, matrix products, on_device(): lax.dot_general(acts_all, lax.all_gather(output_grads, 'row', axis=0, til...  59.5 us
    ppermute x7, waiting for transfers between devices, on_device(): pieces = [lax.ppermute(pieces[0], 'col', hops), *pieces]  56.1 us
    convert_element_type x1, other arithmetic, on_device(): (weight_wide - step_scale / clip_factor * update).astype(jnp.bfloat16)  53.7 us
    psum x1, blocking collectives, on_device(): row_sum, ratio_sum = lax.psum((row_local, ratio_local), ('row', 'col'))  43.2 us
    reduce_sum x1, other arithmetic, on_device(): ratio_local = jnp.sum(squared * inverse * inverse)  28.1 us
    reduce_sum x1, other arithmetic, on_device(): weight_local = jnp.sum(weight_wide * weight_wide)  24.5 us
    psum x1, blocking collectives, on_device(): row_total = lax.psum(row_part, 'col')  22.6 us
  transfers between devices with their start and end apart: 8, of which 7 were waited for; matrix products, arithmetic and copies ran while one was open for 10% of the time, Pallas kernels for 0%

profile of v1, /device:TPU:12, one launch (start us, length us, event | category | flops | bytes accessed | tf_op | source)
XLA Modules:
  0.0 419.8 jit_solution(13385548711136100667)
XLA Ops:
  8.0 9.5 %collective-permute-done = bf16[128,2304]{1,0:T(8,128)(2,1)S(1)} collective-permute-done((bf16[128,2304]{1,0:T(8,128)(2,1)}, bf16[128,2304]{1,0:T(8,128)(2,1)S(1)}, u32[]{:S(2)}, u32[]{:S(2)}) %collective-permute-start) | collective-permute-done | bytes 589856 | tf_op jit(solution)/shard_map/ppermute | solution.py:26
  17.5 9.3 %collective-permute-done.1 = bf16[128,2304]{1,0:T(8,128)(2,1)S(1)} collective-permute-done((bf16[128,2304]{1,0:T(8,128)(2,1)S(1)}, bf16[128,2304]{1,0:T(8,128)(2,1)S(1)}, u32[]{:S(2)}, u32[]{:S(2)}) %collective-permute-start.1) | collective-permute-done | bytes 589856 | tf_op jit(solution)/shard_map/ppermute | solution.py:26
  26.8 9.3 %collective-permute-done.2 = bf16[128,2304]{1,0:T(8,128)(2,1)S(1)} collective-permute-done((bf16[128,2304]{1,0:T(8,128)(2,1)S(1)}, bf16[128,2304]{1,0:T(8,128)(2,1)S(1)}, u32[]{:S(2)}, u32[]{:S(2)}) %collective-permute-start.2) | collective-permute-done | bytes 589856 | tf_op jit(solution)/shard_map/ppermute | solution.py:26
  36.1 9.3 %collective-permute-done.3 = bf16[128,2304]{1,0:T(8,128)(2,1)S(1)} collective-permute-done((bf16[128,2304]{1,0:T(8,128)(2,1)S(1)}, bf16[128,2304]{1,0:T(8,128)(2,1)S(1)}, u32[]{:S(2)}, u32[]{:S(2)}) %collective-permute-start.3) | collective-permute-done | bytes 589856 | tf_op jit(solution)/shard_map/ppermute | solution.py:26
  45.4 9.3 %collective-permute-done.4 = bf16[128,2304]{1,0:T(8,128)(2,1)S(1)} collective-permute-done((bf16[128,2304]{1,0:T(8,128)(2,1)S(1)}, bf16[128,2304]{1,0:T(8,128)(2,1)S(1)}, u32[]{:S(2)}, u32[]{:S(2)}) %collective-permute-start.4) | collective-permute-done | bytes 589856 | tf_op jit(solution)/shard_map/ppermute | solution.py:26
  54.7 9.4 %collective-permute-done.5 = bf16[128,2304]{1,0:T(8,128)(2,1)} collective-permute-done((bf16[128,2304]{1,0:T(8,128)(2,1)S(1)}, bf16[128,2304]{1,0:T(8,128)(2,1)}, u32[]{:S(2)}, u32[]{:S(2)}) %collective-permute-start.5) | collective-permute-done | bytes 589856 | tf_op jit(solution)/shard_map/ppermute | solution.py:26
  64.1 24.5 %fusion = f32[]{:T(128)} fusion(bf16[2304,9216]{1,0:T(8,128)(2,1)} %param.7), kind=kLoop, calls=%fused_computation.3 | loop fusion | flops 63700992 | bytes 42467332 | tf_op jit(solution)/shard_map/reduce_sum | solution.py:19
  88.7 2.1 constant_dynamic-update-slice_fusion.15
  90.8 1.9 constant_dynamic-update-slice_fusion.14
  93.5 0.9 constant_dynamic-update-slice_fusion.12
  94.4 0.9 constant_dynamic-update-slice_fusion.11
  95.2 0.9 constant_dynamic-update-slice_fusion.10
  96.1 0.9 constant_dynamic-update-slice_fusion.9
  96.9 0.9 constant_dynamic-update-slice_fusion.8
  97.8 1.9 constant_dynamic-update-slice_fusion.7
  99.7 1.9 constant_dynamic-update-slice_fusion.6
  101.6 0.9 constant_dynamic-update-slice_fusion.5
  106.7 80.0 %all-gather.2.cloned.1.call-done = bf16[1024,9216]{1,0:T(8,128)(2,1)} async-done(((bf16[256,9216]{1,0:T(8,128)(2,1)}), bf16[1024,9216]{1,0:T(8,128)(2,1)}) %all-gather.2.cloned.1.call-update) | async-done | bytes 18874384 | tf_op jit(solution)/shard_map/all_gather | solution.py:32
  186.8 59.5 %add_reduce_fusion = (f32[9216]{0:T(1024)S(1)}, f32[2304]{0:T(1024)S(1)}, f32[2304,9216]{1,0:T(8,128)}) fusion(bf16[1024,9216]{1,0:T(8,128)(2,1)} %all-gather.2.cloned.1.call-done, bf16[2048,2304]{1,0:T(8,128)(2,1)} %constant_dynamic-update-slice_fusion, s32[]{:T(128)S(6)} %select_n.14), kind=kOutput, calls=%fused_computation.7 | convolution fusion | flops 43571466240 | bytes 108573696 | tf_op jit(solution)/shard_map/dot_general | solution.py:30
  246.3 15.7 %psum.38 = f32[9216]{0:T(1024)S(1)} all-reduce(f32[9216]{0:T(1024)S(1)} %get-tuple-element.3), channel_id=1, replica_groups=mesh['row'=4,'col'=8] {'row'}, use_global_device_ids=true, to_apply=%region_7.8 | all-reduce | flops 9216 | bytes 73728 | tf_op jit(solution)/shard_map/psum | solution.py:40
  262.0 22.6 %psum.36 = f32[2304]{0:T(1024)S(1)} all-reduce(f32[2304]{0:T(1024)S(1)} %get-tuple-element.4), channel_id=1, replica_groups=mesh['row'=4,'col'=8] {'col'}, use_global_device_ids=true, to_apply=%region_3.4 | all-reduce | flops 2304 | bytes 18432 | tf_op jit(solution)/shard_map/psum | solution.py:39
  285.2 28.1 %fusion.2 = f32[]{:T(128)} fusion(f32[2304,9216]{1,0:T(8,128)} %get-tuple-element.10, f32[9216]{0:T(1024)S(1)} %multiply_add_fusion, f32[2304]{0:T(1024)S(1)} %get-tuple-element.9), kind=kLoop, calls=%fused_computation.5 | loop fusion | flops 106168320 | bytes 84980736 | tf_op jit(solution)/shard_map/reduce_sum | solution.py:44
  313.9 43.2 %all-reduce = (f32[]{:T(128)}, f32[]{:T(128)}, f32[]{:T(128)}) all-reduce(f32[]{:T(128)S(6)} %mul.70, f32[]{:T(128)} %fusion, f32[]{:T(128)} %fusion.2), channel_id=1, replica_groups=mesh['row'=4,'col'=8] {'row','col'}, use_global_device_ids=true, to_apply=%region_5.6 | all-reduce | flops 3 | bytes 24 | tf_op jit(solution)/shard_map/psum | solution.py:47
  359.2 53.7 %fusion.1 = bf16[2304,9216]{1,0:T(8,128)(2,1)} fusion(bf16[2304,9216]{1,0:T(8,128)(2,1)} %param.7, f32[2304,9216]{1,0:T(8,128)} %get-tuple-element.10, f32[]{:T(128)S(6)} %sqrt.11, f32[]{:T(128)S(6)} %div.32, f32[9216]{0:T(1024)S(1)} %multiply_add_fusion, f32[2304]{0:T(1024)S(1)} %get-tuple-element.9), kind=kLoop, calls=%fused_computation.4 | loop fusion | flops 148635648 | bytes 169915392 | tf_op jit(solution)/shard_map/convert_element_type | solution.py:53
  (28 shorter events, 6.5 us)
Async XLA Ops:
  7.2 179.6 %all-gather.2.cloned.1.call-start = ((), (), s32[]{:S(2)}) async-start(), calls=%async_computation | async-start | bytes 23592960 | tf_op jit(solution)/shard_map/all_gather | solution.py:32
  7.9 89.0 %copy-start = (bf16[128,2304]{1,0:T(8,128)(2,1)S(1)}, bf16[128,2304]{1,0:T(8,128)(2,1)}, u32[]{:S(2)}) copy-start(bf16[128,2304]{1,0:T(8,128)(2,1)} %param.5) | copy-start | bytes 1769476
  7.9 9.6 %collective-permute-start = (bf16[128,2304]{1,0:T(8,128)(2,1)}, bf16[128,2304]{1,0:T(8,128)(2,1)S(1)}, u32[]{:S(2)}, u32[]{:S(2)}) collective-permute-start(bf16[128,2304]{1,0:T(8,128)(2,1)} %param.5), channel_id=1, source_target_pairs={{0,1},{1,2},{2,3},{3,4},{4,5},{5,6},{6,7},{7,0},{8,9},{9,10},{10,1... | collective-permute-start | bytes 1769480 | tf_op jit(solution)/shard_map/ppermute | solution.py:26
  17.5 9.3 %collective-permute-start.1 = (bf16[128,2304]{1,0:T(8,128)(2,1)S(1)}, bf16[128,2304]{1,0:T(8,128)(2,1)S(1)}, u32[]{:S(2)}, u32[]{:S(2)}) collective-permute-start(bf16[128,2304]{1,0:T(8,128)(2,1)S(1)} %collective-permute-done), channel_id=1, source_target_pairs={{0,1},{1,2},{2,3},{3,4},{4,5},{5,6},{6,7},{7,0},{8,9},{9,10},{10,1... | collective-permute-start | bytes 1769480 | tf_op jit(solution)/shard_map/ppermute | solution.py:26
  26.8 9.3 %collective-permute-start.2 = (bf16[128,2304]{1,0:T(8,128)(2,1)S(1)}, bf16[128,2304]{1,0:T(8,128)(2,1)S(1)}, u32[]{:S(2)}, u32[]{:S(2)}) collective-permute-start(bf16[128,2304]{1,0:T(8,128)(2,1)S(1)} %collective-permute-done.1), channel_id=1, source_target_pairs={{0,1},{1,2},{2,3},{3,4},{4,5},{5,6},{6,7},{7,0},{8,9},{9,10},{10,1... | collective-permute-start | bytes 1769480 | tf_op jit(solution)/shard_map/ppermute | solution.py:26
  36.1 9.3 %collective-permute-start.3 = (bf16[128,2304]{1,0:T(8,128)(2,1)S(1)}, bf16[128,2304]{1,0:T(8,128)(2,1)S(1)}, u32[]{:S(2)}, u32[]{:S(2)}) collective-permute-start(bf16[128,2304]{1,0:T(8,128)(2,1)S(1)} %collective-permute-done.2), channel_id=1, source_target_pairs={{0,1},{1,2},{2,3},{3,4},{4,5},{5,6},{6,7},{7,0},{8,9},{9,10},{10,1... | collective-permute-start | bytes 1769480 | tf_op jit(solution)/shard_map/ppermute | solution.py:26
  45.4 9.3 %collective-permute-start.4 = (bf16[128,2304]{1,0:T(8,128)(2,1)S(1)}, bf16[128,2304]{1,0:T(8,128)(2,1)S(1)}, u32[]{:S(2)}, u32[]{:S(2)}) collective-permute-start(bf16[128,2304]{1,0:T(8,128)(2,1)S(1)} %collective-permute-done.3), channel_id=1, source_target_pairs={{0,1},{1,2},{2,3},{3,4},{4,5},{5,6},{6,7},{7,0},{8,9},{9,10},{10,1... | collective-permute-start | bytes 1769480 | tf_op jit(solution)/shard_map/ppermute | solution.py:26
  54.7 9.4 %collective-permute-start.5 = (bf16[128,2304]{1,0:T(8,128)(2,1)S(1)}, bf16[128,2304]{1,0:T(8,128)(2,1)}, u32[]{:S(2)}, u32[]{:S(2)}) collective-permute-start(bf16[128,2304]{1,0:T(8,128)(2,1)S(1)} %collective-permute-done.4), channel_id=1, source_target_pairs={{0,1},{1,2},{2,3},{3,4},{4,5},{5,6},{6,7},{7,0},{8,9},{9,10},{10,1... | collective-permute-start | bytes 1769480 | tf_op jit(solution)/shard_map/ppermute | solution.py:26
  64.1 24.5 %collective-permute-start.6 = (bf16[128,2304]{1,0:T(8,128)(2,1)}, bf16[128,2304]{1,0:T(8,128)(2,1)}, u32[]{:S(2)}, u32[]{:S(2)}) collective-permute-start(bf16[128,2304]{1,0:T(8,128)(2,1)} %collective-permute-done.5), channel_id=1, source_target_pairs={{0,1},{1,2},{2,3},{3,4},{4,5},{5,6},{6,7},{7,0},{8,9},{9,10},{10,1... | collective-permute-start | bytes 1769480 | tf_op jit(solution)/shard_map/ppermute | solution.py:26
  106.7 177.8 %copy-start.3 = (f32[9216]{0:T(1024)S(1)}, f32[9216]{0:T(1024)}, u32[]{:S(2)}) copy-start(f32[9216]{0:T(1024)} %param.9) | copy-start | bytes 110596
  106.7 177.8 %copy-start.4 = (f32[2304]{0:T(1024)S(1)}, f32[2304]{0:T(1024)}, u32[]{:S(2)}) copy-start(f32[2304]{0:T(1024)} %param.8) | copy-start | bytes 27652
  284.6 74.6 %copy-start.1 = (f32[9216]{0:T(1024)}, f32[9216]{0:T(1024)S(1)}, u32[]{:S(2)}) copy-start(f32[9216]{0:T(1024)S(1)} %multiply_add_fusion) | copy-start | bytes 110596
  285.2 74.0 %copy-start.2 = (f32[2304]{0:T(1024)}, f32[2304]{0:T(1024)S(1)}, u32[]{:S(2)}) copy-start(f32[2304]{0:T(1024)S(1)} %get-tuple-element.9) | copy-start | bytes 27652
Sparse Core Ops, SparseCore 0:
  9.8 176.9 all-gather.1
